TPU v7x, 32 devices: a whole 2x2x4 slice. The times are simulated.
32 devices in a mesh: row: 4 (over y, x), col: 8 (over z, core).
Axes of the slice: x: 2, y: 2, z: 4, core: 2. Of those that a mesh axis runs over, the one named last changes fastest.
Arguments:
- view_one: bfloat16 [2048, 8192], P('row', 'col'), may hold values from -6 to 6
- view_two: bfloat16 [2048, 8192], P('row', 'col'), may hold values from -6 to 6
- pair_weights: bfloat16 [8192, 8192], P('row', 'col'), may hold values from 0.25 to 2.5
Outputs:
- first_grad: bfloat16 [2048, 8192], P('row', 'col')
- second_grad: bfloat16 [2048, 8192], P('row', 'col')
All inputs are finite; a program needn't handle non-finite values.
Results may differ from a plain program's by a relative error of at most 0.004.
Values may be sent and summed in bfloat16 or wider, within the bound.
A program may use at most 128 MiB of HBM per device.

v0:
```python
import jax
import jax.numpy as jnp
from jax import lax
from jax.sharding import PartitionSpec as P


def per_device(view_one, view_two, pair_weights):
    wide_two = lax.all_gather(view_two, "col", axis=1, tiled=True)
    samples = view_one.shape[0] * lax.axis_size("row")
    local_rows = pair_weights.shape[0]
    local_cols = pair_weights.shape[1]
    regrouped = lax.all_to_all(wide_two, "row", split_axis=1, concat_axis=0, tiled=True)
    summed = lax.dot_general(
        regrouped,
        lax.all_gather(view_one, "row", axis=0, tiled=True),
        (((0,), (0,)), ((), ())),
        preferred_element_type=jnp.float32,
    )
    correlation = summed / samples
    row_ids = lax.axis_index("row") * local_rows + lax.broadcasted_iota(
        jnp.int32, (local_rows, local_cols), 0
    )
    col_ids = lax.axis_index("col") * local_cols + lax.broadcasted_iota(
        jnp.int32, (local_rows, local_cols), 1
    )
    identity = jnp.where(row_ids == col_ids, 1.0, 0.0).astype(jnp.float32)
    weighted = (pair_weights.astype(jnp.float32) * (correlation - identity)).astype(jnp.bfloat16)
    grad_cols = lax.all_gather(weighted, "row", axis=0, tiled=True)
    first_grad = jnp.dot(wide_two, grad_cols, preferred_element_type=jnp.float32).astype(
        jnp.bfloat16
    )
    second_flipped = lax.psum_scatter(
        lax.dot_general(
            grad_cols, view_one, (((1,), (1,)), ((), ())), preferred_element_type=jnp.float32
        ),
        "col",
        scatter_dimension=0,
        tiled=True,
    )
    return (first_grad, second_flipped.T.astype(jnp.bfloat16))


def solution(mesh):
    placed = (P("row", "col"), P("row", "col"), P("row", "col"))
    return jax.shard_map(
        per_device,
        mesh=mesh,
        in_specs=placed,
        out_specs=(P("row", "col"), P("row", "col")),
        check_vma=False,
    )
```

profile of v0, /device:TPU:0, one launch (start us, length us, event | category | flops | bytes accessed | tf_op | source)
XLA Modules:
  0.0 604.9 jit_solution(17463055193101031785)
XLA Ops:
  8.0 0.0 all-gather.4.cloned.1.call-start
  8.0 2.3 copy.9
  10.3 0.0 all-gather.4.cloned.1.call-update
  10.3 85.4 %all-gather.4.cloned.1.call-done = bf16[512,8192]{0,1:T(8,128)(2,1)} async-done(((bf16[512,1024]{0,1:T(8,128)(2,1)}), bf16[512,8192]{0,1:T(8,128)(2,1)}) %all-gather.4.cloned.1.call-update) | async-done | bytes 8388624 | tf_op jit(solution)/shard_map/all_gather | solution.py:8
  95.8 5.7 all-to-all-start
  101.4 0.0 all-gather.6.cloned.1.call-start
  101.5 0.5 all-gather.6.cloned.1.call-update
  102.0 0.0 all-gather.8.cloned.1.call-start
  102.1 126.1 %all-to-all-done = bf16[512,4,2048]{0,2,1:T(8,128)(2,1)} async-done(((bf16[512,4,2048]{0,2,1:T(8,128)(2,1)}), bf16[512,4,2048]{0,2,1:T(8,128)(2,1)}, u32[]{:S(2)}, u32[]{:S(2)}) %all-to-all-start) | async-done | bytes 8388640 | tf_op jit(solution)/shard_map/all_to_all | solution.py:12
  228.2 11.4 %copy.10 = bf16[4,512,2048]{2,1,0:T(8,128)(2,1)} copy(bf16[4,512,2048]{1,2,0:T(8,128)(2,1)} %bitcast.1) | data formatting | bytes 16777216 | tf_op jit(solution)/shard_map/all_to_all | solution.py:12
  239.6 0.0 all-gather.6.cloned.1.call-done
  239.6 0.0 copy-start
  239.6 15.8 %multiply_convert_fusion = bf16[2048,1024]{1,0:T(8,128)(2,1)} fusion(bf16[2048,1024]{1,0:T(8,128)(2,1)} %param.5, bf16[2048,2048]{1,0:T(8,128)(2,1)} %bitcast.14, bf16[2048,1024]{1,0:T(8,128)(2,1)} %all-gather.6.cloned.1.call-done, s32[1024]{0:T(1024)S(1)} %iota_add_fusion.1, s32[2048]{0:T(1024)S(1)} %iota_add_fusion), kind=kOutput, calls=%fused_computation | convolution fusion | flops 8604614656 | bytes 20983808 | tf_op jit(solution)/shard_map/dot_general | solution.py:13
  255.4 0.0 all-gather.8.cloned.1.call-update
  255.4 0.2 reduce-scatter.2.cloned.1.call-start
  255.7 154.6 %all-gather.8.cloned.1.call-done = bf16[8192,1024]{1,0:T(8,128)(2,1)} async-done(((bf16[2048,1024]{1,0:T(8,128)(2,1)}), bf16[8192,1024]{1,0:T(8,128)(2,1)}) %all-gather.8.cloned.1.call-update) | async-done | bytes 16777232 | tf_op jit(solution)/shard_map/all_gather | solution.py:28
  410.3 0.0 copy-done
  410.3 15.8 %fusion.1 = f32[8192,512]{1,0:T(8,128)} fusion(bf16[8192,1024]{1,0:T(8,128)(2,1)} %all-gather.8.cloned.1.call-done, bf16[512,1024]{1,0:T(8,128)(2,1)S(1)} %copy-done), kind=kOutput, calls=%fused_computation.6 | convolution fusion | flops 8589934592 | bytes 34603008 | tf_op jit(solution)/shard_map/dot_general | solution.py:33
  426.0 0.0 reduce-scatter.2.cloned.1.call-update
  426.1 14.8 %fusion = bf16[512,1024]{0,1:T(8,128)(2,1)S(1)} fusion(bf16[8192,1024]{1,0:T(8,128)(2,1)} %all-gather.8.cloned.1.call-done, bf16[512,8192]{0,1:T(8,128)(2,1)} %all-gather.4.cloned.1.call-done), kind=kOutput, calls=%fused_computation.2 | convolution fusion | flops 8590458880 | bytes 26214400 | tf_op jit(solution)/shard_map/dot_general | solution.py:29
  440.9 1.3 copy.11
  442.2 152.2 %reduce-scatter.2.cloned.1.call-done = f32[1024,512]{1,0:T(8,128)} async-done(((f32[8192,512]{1,0:T(8,128)}), f32[1024,512]{1,0:T(8,128)}) %reduce-scatter.2.cloned.1.call-update) | async-done | bytes 2097168 | tf_op jit(solution)/shard_map/reduce_scatter | solution.py:32
  594.4 1.7 convert_bitcast_fusion
  596.1 1.3 copy.12
  (2 shorter events, 0.0 us)
Async XLA Ops:
  8.0 87.8 %all-gather.4.cloned.1.call-start = ((), (), s32[]{:S(2)}) async-start(), calls=%async_computation.2 | async-start | bytes 9437184 | tf_op jit(solution)/shard_map/all_gather | solution.py:8
  95.8 132.4 %all-to-all-start = ((bf16[512,4,2048]{0,2,1:T(8,128)(2,1)}), bf16[512,4,2048]{0,2,1:T(8,128)(2,1)}, u32[]{:S(2)}, u32[]{:S(2)}) async-start(bf16[512,4,2048]{0,2,1:T(8,128)(2,1)} %bitcast.13), calls=%async_computation | async-start | bytes 16777216 | tf_op jit(solution)/shard_map/all_to_all | solution.py:12
  101.4 138.2 %all-gather.6.cloned.1.call-start = ((), (), s32[]{:S(2)}) async-start(), calls=%async_computation.3 | async-start | bytes 5242880 | tf_op jit(solution)/shard_map/all_gather | solution.py:15
  102.0 308.3 %all-gather.8.cloned.1.call-start = ((), (), s32[]{:S(2)}) async-start(), calls=%async_computation.4 | async-start | bytes 20971520 | tf_op jit(solution)/shard_map/all_gather | solution.py:28
  239.6 170.7 %copy-start = (bf16[512,1024]{1,0:T(8,128)(2,1)S(1)}, bf16[512,1024]{1,0:T(8,128)(2,1)}, u32[]{:S(2)}) copy-start(bf16[512,1024]{1,0:T(8,128)(2,1)} %param.3) | copy-start | bytes 3145732
  255.4 339.0 %reduce-scatter.2.cloned.1.call-start = ((), (), s32[]{:S(2)}) async-start(), calls=%async_computation.5 | async-start | bytes 18874368 | tf_op jit(solution)/shard_map/reduce_scatter | solution.py:32
Sparse Core Ops, SparseCore 0:
  11.0 84.7 all-gather.3
  426.2 168.1 reduce-scatter.1
Sparse Core Ops, SparseCore 1:
  103.8 118.6 all-gather.5
  255.5 154.7 all-gather.7
where the time goes:
time: 605 us
  waiting for transfers between devices  519 us (86%)
  matrix products  46.4 us (8%)
  local copies, waits for them, and re-layouts  16.3 us (3%)
  between operations  15.5 us (3%)
    all_gather x1, waiting for transfers between devices, per_device(): grad_cols = lax.all_gather(weighted, 'row', axis=0, tiled=True)  155 us
    reduce_scatter x1, waiting for transfers between devices, per_device(): lax.psum_scatter(lax.dot_general(grad_cols, view_one, (((1,), (1,)), ((),...  152 us
    all_to_all x1, waiting for transfers between devices, per_device(): lax.all_to_all(wide_two, 'row', split_axis=1, concat_axis=0, tiled=True)  126 us
    all_gather x1, waiting for transfers between devices, per_device(): wide_two = lax.all_gather(view_two, 'col', axis=1, tiled=True)  85.4 us
    dot_general x1, matrix products, per_device(): lax.dot_general(regrouped, lax.all_gather(view_one, 'row', axis=0, tiled=...  15.8 us
    dot_general x1, matrix products, per_device(): lax.dot_general(grad_cols, view_one, (((1,), (1,)), ((), ())), preferred_...  15.8 us
    dot_general x1, matrix products, per_device(): jnp.dot(wide_two, grad_cols, preferred_element_type=jnp.float32)  14.8 us
  transfers between devices with their start and end apart: 5, of which 4 were waited for; matrix products, arithmetic and copies ran while one was open for 5% of the time, Pallas kernels for 0%

commit v1 on v0

--- a/solution.py
+++ b/solution.py
@@ -4,8 +4,13 @@
 from jax.sharding import PartitionSpec as P
 
 
+def handle_plate(vec):
+    local_next = jnp.concatenate(lax.all_gather(vec, axis_name="col"), axis=1)
+    return local_next
+
+
 def per_device(view_one, view_two, pair_weights):
-    wide_two = lax.all_gather(view_two, "col", axis=1, tiled=True)
+    wide_two = handle_plate(view_two)
     samples = view_one.shape[0] * lax.axis_size("row")
     local_rows = pair_weights.shape[0]
     local_cols = pair_weights.shape[1]

time: 605 us -> 616 us (1.018)
  local copies, waits for them, and re-layouts: 16.3 us -> 25.5 us
    reshape x0 -> x1, local copies, waits for them, and re-layouts: none -> 11.4 us  [handle_plate(): local_next = jnp.concatenate(lax.all_gather(vec, axis_name='col'), axis=1)]
  transfers between devices with their start and end apart: 5 -> 5, of which waited for: 4 -> 4; matrix products, arithmetic and copies ran while one was open for 5% -> 4% of each run, Pallas kernels for 0% -> 0%
where the time goes in v1:
time: 616 us
  waiting for transfers between devices  521 us (85%)
  matrix products  46.4 us (8%)
  local copies, waits for them, and re-layouts  25.5 us (4%)
  between operations  15.5 us (3%)
    all_gather x1, waiting for transfers between devices, per_device(): grad_cols = lax.all_gather(weighted, 'row', axis=0, tiled=True)  155 us
    reduce_scatter x1, waiting for transfers between devices, per_device(): lax.psum_scatter(lax.dot_general(grad_cols, view_one, (((1,), (1,)), ((),...  152 us
    all_to_all x1, waiting for transfers between devices, per_device(): lax.all_to_all(wide_two, 'row', split_axis=1, concat_axis=0, tiled=True)  126 us
    all_gather x1, waiting for transfers between devices, handle_plate(): local_next = jnp.concatenate(lax.all_gather(vec, axis_name='col'), axis=1)  86.5 us
    dot_general x1, matrix products, per_device(): lax.dot_general(regrouped, lax.all_gather(view_one, 'row', axis=0, tiled=...  15.8 us
    dot_general x1, matrix products, per_device(): lax.dot_general(grad_cols, view_one, (((1,), (1,)), ((), ())), preferred_...  15.8 us
    dot_general x1, matrix products, per_device(): jnp.dot(wide_two, grad_cols, preferred_element_type=jnp.float32)  14.8 us
  transfers between devices with their start and end apart: 5, of which 4 were waited for; matrix products, arithmetic and copies ran while one was open for 4% of the time, Pallas kernels for 0%

profile of v1, /device:TPU:0, one launch (start us, length us, event | category | flops | bytes accessed | tf_op | source)
XLA Modules:
  0.0 615.7 jit_solution(1238888336469507438)
XLA Ops:
  8.0 0.0 all-gather.9.cloned.1.call-start
  8.0 0.7 all-gather.9.cloned.1.call-update
  8.7 86.5 %all-gather.9.cloned.1.call-done = bf16[4096,1024]{1,0:T(8,128)(2,1)} async-done(((bf16[512,1024]{1,0:T(8,128)(2,1)}), bf16[4096,1024]{1,0:T(8,128)(2,1)}) %all-gather.9.cloned.1.call-update) | async-done | bytes 8388624 | tf_op jit(solution)/shard_map/all_gather | solution.py:8
  95.2 11.4 %copy.10 = bf16[512,8,1024]{0,2,1:T(8,128)(2,1)} copy(bf16[512,8,1024]{2,0,1:T(8,128)(2,1)} %bitcast.19) | data formatting | bytes 16777216 | tf_op jit(solution)/shard_map/reshape | solution.py:8
  106.6 5.7 all-to-all-start
  112.3 0.0 all-gather.5.cloned.1.call-start
  112.3 0.5 all-gather.5.cloned.1.call-update
  112.9 0.0 all-gather.7.cloned.1.call-start
  112.9 126.1 %all-to-all-done = bf16[512,4,2048]{0,2,1:T(8,128)(2,1)} async-done(((bf16[512,4,2048]{0,2,1:T(8,128)(2,1)}), bf16[512,4,2048]{0,2,1:T(8,128)(2,1)}, u32[]{:S(2)}, u32[]{:S(2)}) %all-to-all-start) | async-done | bytes 8388640 | tf_op jit(solution)/shard_map/all_to_all | solution.py:17
  239.0 11.4 %copy.11 = bf16[4,512,2048]{2,1,0:T(8,128)(2,1)} copy(bf16[4,512,2048]{1,2,0:T(8,128)(2,1)} %bitcast.3) | data formatting | bytes 16777216 | tf_op jit(solution)/shard_map/all_to_all | solution.py:17
  250.4 0.0 all-gather.5.cloned.1.call-done
  250.4 0.0 copy-start
  250.4 15.8 %multiply_convert_fusion = bf16[2048,1024]{1,0:T(8,128)(2,1)} fusion(bf16[2048,1024]{1,0:T(8,128)(2,1)} %param.5, bf16[2048,2048]{1,0:T(8,128)(2,1)} %bitcast.20, bf16[2048,1024]{1,0:T(8,128)(2,1)} %all-gather.5.cloned.1.call-done, s32[1024]{0:T(1024)S(1)} %iota_add_fusion.1, s32[2048]{0:T(1024)S(1)} %iota_add_fusion), kind=kOutput, calls=%fused_computation | convolution fusion | flops 8604614656 | bytes 20983808 | tf_op jit(solution)/shard_map/dot_general | solution.py:18
  266.3 0.0 all-gather.7.cloned.1.call-update
  266.3 0.2 reduce-scatter.2.cloned.1.call-start
  266.5 154.6 %all-gather.7.cloned.1.call-done = bf16[8192,1024]{1,0:T(8,128)(2,1)} async-done(((bf16[2048,1024]{1,0:T(8,128)(2,1)}), bf16[8192,1024]{1,0:T(8,128)(2,1)}) %all-gather.7.cloned.1.call-update) | async-done | bytes 16777232 | tf_op jit(solution)/shard_map/all_gather | solution.py:33
  421.1 0.0 copy-done
  421.1 15.8 %fusion.1 = f32[8192,512]{1,0:T(8,128)} fusion(bf16[8192,1024]{1,0:T(8,128)(2,1)} %all-gather.7.cloned.1.call-done, bf16[512,1024]{1,0:T(8,128)(2,1)S(1)} %copy-done), kind=kOutput, calls=%fused_computation.6 | convolution fusion | flops 8589934592 | bytes 34603008 | tf_op jit(solution)/shard_map/dot_general | solution.py:38
  436.9 0.0 reduce-scatter.2.cloned.1.call-update
  436.9 14.8 %fusion = bf16[512,1024]{0,1:T(8,128)(2,1)S(1)} fusion(bf16[8192,1024]{1,0:T(8,128)(2,1)} %all-gather.7.cloned.1.call-done, bf16[512,8192]{0,1:T(8,128)(2,1)} %bitcast.18), kind=kOutput, calls=%fused_computation.2 | convolution fusion | flops 8590458880 | bytes 26214400 | tf_op jit(solution)/shard_map/dot_general | solution.py:34
  451.7 1.3 copy.13
  453.1 152.2 %reduce-scatter.2.cloned.1.call-done = f32[1024,512]{1,0:T(8,128)} async-done(((f32[8192,512]{1,0:T(8,128)}), f32[1024,512]{1,0:T(8,128)}) %reduce-scatter.2.cloned.1.call-update) | async-done | bytes 2097168 | tf_op jit(solution)/shard_map/reduce_scatter | solution.py:37
  605.2 1.7 convert_bitcast_fusion
  607.0 1.3 copy.14
  (2 shorter events, 0.0 us)
Async XLA Ops:
  8.0 87.2 %all-gather.9.cloned.1.call-start = ((), (), s32[]{:S(2)}) async-start(), calls=%async_computation.5 | async-start | bytes 9437184 | tf_op jit(solution)/shard_map/all_gather | solution.py:8
  106.6 132.4 %all-to-all-start = ((bf16[512,4,2048]{0,2,1:T(8,128)(2,1)}), bf16[512,4,2048]{0,2,1:T(8,128)(2,1)}, u32[]{:S(2)}, u32[]{:S(2)}) async-start(bf16[512,4,2048]{0,2,1:T(8,128)(2,1)} %bitcast.17), calls=%async_computation | async-start | bytes 16777216 | tf_op jit(solution)/shard_map/all_to_all | solution.py:17
  112.3 138.2 %all-gather.5.cloned.1.call-start = ((), (), s32[]{:S(2)}) async-start(), calls=%async_computation.2 | async-start | bytes 5242880 | tf_op jit(solution)/shard_map/all_gather | solution.py:20
  112.9 308.3 %all-gather.7.cloned.1.call-start = ((), (), s32[]{:S(2)}) async-start(), calls=%async_computation.3 | async-start | bytes 20971520 | tf_op jit(solution)/shard_map/all_gather | solution.py:33
  250.4 170.7 %copy-start = (bf16[512,1024]{1,0:T(8,128)(2,1)S(1)}, bf16[512,1024]{1,0:T(8,128)(2,1)}, u32[]{:S(2)}) copy-start(bf16[512,1024]{1,0:T(8,128)(2,1)} %param.3) | copy-start | bytes 3145732
  266.3 339.0 %reduce-scatter.2.cloned.1.call-start = ((), (), s32[]{:S(2)}) async-start(), calls=%async_computation.4 | async-start | bytes 18874368 | tf_op jit(solution)/shard_map/reduce_scatter | solution.py:37
Sparse Core Ops, SparseCore 0:
  10.4 84.7 all-gather.8
  437.0 168.1 reduce-scatter.1
Sparse Core Ops, SparseCore 1:
  114.6 118.6 all-gather.4
  266.4 154.7 all-gather.6
